TPU v7x, 32 devices: a whole 2x2x4 slice. The times are simulated.
32 devices in a mesh: sec: 2 (over x), tile: 16 (over z, y, core).
Axes of the slice: x: 2, y: 2, z: 4, core: 2. Of those that a mesh axis runs over, the one named last changes fastest.
Arguments:
- atmosphere: bfloat16 [32, 360, 384], P(('sec', 'tile')), may hold values from -6 to 6
- ocean_state: bfloat16 [128, 1440, 128], P('tile', 'sec'), may hold values from -6 to 6
- land_mask: int32 [128, 1440], P('tile', 'sec'), may hold values 0 or 1
- crossing_bands: int32 [16, 4], P('tile'), may hold values from 0 to 31, as said below
- ocean_regrid: float32 [16, 4, 8, 1], P('tile'), may hold values from 0 to 1, as said below
- atmosphere_regrid: float32 [16, 4, 1, 8], P('tile'), may hold values from 0 to 1, as said below
- surface_read: bfloat16 [128], replicated, may hold values from -0.5 to 0.5
- surface_embed: float32 [384], replicated, may hold values from -4 to 4
- flux_read: bfloat16 [384, 8], replicated, may hold values from -0.3125 to 0.3125
- flux_embed: bfloat16 [8, 128], replicated, may hold values from -2 to 2
- legendre_forward: bfloat16 [128, 32, 32], P(('sec', 'tile')), may hold values from -1 to 1
- legendre_inverse: bfloat16 [128, 32, 32], P(('sec', 'tile')), may hold values from -1 to 1
- spectral_mix: bfloat16 [2, 384, 384], replicated, may hold values from -0.3125 to 0.3125
- conv_kernel: bfloat16 [2, 7, 7, 128], replicated, may hold values from -0.875 to 0.875
- norm_gain: float32 [2, 128], replicated, may hold values from 0.1 to 1.9
- expand_weight: bfloat16 [2, 128, 512], replicated, may hold values from -0.5 to 0.5
- project_weight: bfloat16 [2, 512, 128], replicated, may hold values from -0.25 to 0.25
- atmosphere_cotangent: bfloat16 [32, 360, 384], P(('sec', 'tile')), may hold values from -6 to 6
- ocean_cotangent: bfloat16 [128, 1440, 128], P('tile', 'sec'), may hold values from -6 to 6
Outputs:
- atmosphere_next: bfloat16 [32, 360, 384], P(('sec', 'tile'))
- ocean_next: bfloat16 [128, 1440, 128], P('tile', 'sec')
- atmosphere_grad: float32 [32, 360, 384], P(('sec', 'tile'))
- ocean_grad: float32 [128, 1440, 128], P('tile', 'sec')
Inputs may be any that keep to these rules, and one draw needn't show every extreme that they name: `crossing_bands`: row j lists between 1 and 4 consecutive distinct atmosphere bands, then repeats its last band; some row lists 4. Its first band is j * 2 - 1, j * 2 or j * 2 + 1, raised to 0 or lowered as far as needed for the list to end at band 32 - 1 at most. `ocean_regrid`: zero in the repeated slots of crossing_bands; the entries of each ocean row sum to one. `atmosphere_regrid`: zero in the repeated slots of crossing_bands.
All inputs are finite; a program needn't handle non-finite values. No bound on the sum of `land_mask` on one device may be relied on, other than what follows from the above.
Results may differ from a plain program's by a relative error of at most 0.008.
Values may be sent and summed in bfloat16 or wider, within the bound.
A program may use at most 128 MiB of HBM per device.

v0:
```python
import jax
import jax.numpy as jnp
from jax import lax
from jax.sharding import PartitionSpec as P


def with_halo(x, sides, width, wrap):
    for axis, dim in sides:
        size, length = (lax.axis_size(axis), x.shape[dim])
        up = [(i, (i + 1) % size) for i in range(size if wrap else size - 1)]
        down = [(j, i) for i, j in up]
        last = lax.slice_in_dim(x, length - width, length, axis=dim)
        first = lax.slice_in_dim(x, 0, width, axis=dim)
        before = lax.ppermute(last, axis, up)
        after = lax.ppermute(first, axis, down)
        x = jnp.concatenate([before, x, after], axis=dim)
    return x


def wave_table(lon_count, mode_count):
    longitude = jnp.arange(lon_count, dtype=jnp.int32)
    wavenumber = jnp.arange(mode_count, dtype=jnp.int32)
    phase = (longitude[:, None] * wavenumber[None, :] % lon_count).astype(jnp.float32) * (
        2.0 * jnp.pi / lon_count
    )
    scaled = jnp.stack([jnp.cos(phase), -jnp.sin(phase)], axis=2) * jnp.sqrt(
        jnp.float32(2.0 / lon_count)
    )
    return scaled.reshape(lon_count, 2 * mode_count).astype(jnp.bfloat16)


def depthwise(window, kernel):
    radius = kernel.shape[0] // 2
    height = window.shape[0] - 2 * radius
    extent = window.shape[1] - 2 * radius
    wide = window.astype(jnp.float32)
    weights = kernel.astype(jnp.float32)
    total = jnp.zeros((height, extent, window.shape[2]), jnp.float32)
    for shift_row in range(kernel.shape[0]):
        for shift_col in range(kernel.shape[1]):
            total = (
                total
                + wide[shift_row : shift_row + height, shift_col : shift_col + extent]
                * weights[shift_row, shift_col]
            )
    return total


def cell_forward(hidden, gain, expand, project):
    center = hidden - jnp.mean(hidden, axis=-1, keepdims=True)
    inverse_std = lax.rsqrt(jnp.mean(center * center, axis=-1, keepdims=True) + 1e-06)
    normed = (center * inverse_std * gain).astype(jnp.bfloat16)
    before = jnp.dot(normed, expand, preferred_element_type=jnp.float32)
    active = jax.nn.gelu(before).astype(jnp.bfloat16)
    return jnp.dot(active, project, preferred_element_type=jnp.float32)


def cell_backward(hidden, gain, expand, project, mask_value, cotangent):
    center = hidden - jnp.mean(hidden, axis=-1, keepdims=True)
    inverse_std = lax.rsqrt(jnp.mean(center * center, axis=-1, keepdims=True) + 1e-06)
    unit = center * inverse_std
    normed = (unit * gain).astype(jnp.bfloat16)
    before = jnp.dot(normed, expand, preferred_element_type=jnp.float32)
    masked = (mask_value[:, :, None] * cotangent).astype(jnp.bfloat16)
    active_adjoint = jnp.dot(masked, project.T, preferred_element_type=jnp.float32)
    _, gelu_back = jax.vjp(jax.nn.gelu, before)
    before_adjoint = gelu_back(active_adjoint)[0].astype(jnp.bfloat16)
    normed_adjoint = jnp.dot(before_adjoint, expand.T, preferred_element_type=jnp.float32)
    scaled = normed_adjoint * gain
    result = inverse_std * (
        scaled
        - jnp.mean(scaled, axis=-1, keepdims=True)
        - unit * jnp.mean(scaled * unit, axis=-1, keepdims=True)
    )
    return result.astype(jnp.bfloat16)


def ocean_matrix(bands_row, blocks, lat_count):
    lat_band = blocks.shape[2]
    index = bands_row[:, None] * lat_band + jnp.arange(lat_band, dtype=jnp.int32)[None, :]
    onehot = (index[:, :, None] == jnp.arange(lat_count, dtype=jnp.int32)[None, None, :]).astype(
        jnp.float32
    )
    return jnp.einsum("poi,pia->oa", blocks, onehot, precision=lax.Precision.HIGHEST)


def atmosphere_matrix(bands_row, blocks, lat_count):
    lat_band = blocks.shape[1]
    index = bands_row[:, None] * lat_band + jnp.arange(lat_band, dtype=jnp.int32)[None, :]
    onehot = (index[:, :, None] == jnp.arange(lat_count, dtype=jnp.int32)[None, None, :]).astype(
        jnp.float32
    )
    return jnp.einsum("pio,pia->ao", blocks, onehot, precision=lax.Precision.HIGHEST)


def mix_complex(coefficient, mix_real, mix_imag):
    real_part = coefficient[:, :, 0]
    imag_part = coefficient[:, :, 1]
    out_real = jnp.einsum(
        "lmc,cd->lmd", real_part, mix_real, preferred_element_type=jnp.float32
    ) - jnp.einsum("lmc,cd->lmd", imag_part, mix_imag, preferred_element_type=jnp.float32)
    out_imag = jnp.einsum(
        "lmc,cd->lmd", imag_part, mix_real, preferred_element_type=jnp.float32
    ) + jnp.einsum("lmc,cd->lmd", real_part, mix_imag, preferred_element_type=jnp.float32)
    return jnp.stack([out_real, out_imag], axis=2).astype(jnp.bfloat16)


def spectral_block(spectrum, forward, inverse, mixing):
    lat_count, columns, channels = spectrum.shape
    split = spectrum.reshape(lat_count, columns // 2, 2, channels)
    coefficient = jnp.einsum(
        "mla,amrc->lmrc", forward, split, preferred_element_type=jnp.float32
    ).astype(jnp.bfloat16)
    mixed = mix_complex(coefficient, mixing[0], mixing[1])
    returned = jnp.einsum(
        "mal,lmrc->amrc", inverse, mixed, preferred_element_type=jnp.float32
    ).astype(jnp.bfloat16)
    return returned.reshape(lat_count, columns, channels)


def spectral_adjoint(returned_adjoint, forward, inverse, mixing):
    lat_count, columns, channels = returned_adjoint.shape
    split = returned_adjoint.reshape(lat_count, columns // 2, 2, channels)
    mixed_adjoint = jnp.einsum(
        "mal,amrc->lmrc", inverse, split, preferred_element_type=jnp.float32
    ).astype(jnp.bfloat16)
    real_part = mixed_adjoint[:, :, 0]
    imag_part = mixed_adjoint[:, :, 1]
    back_real = jnp.einsum(
        "lmd,cd->lmc", real_part, mixing[0], preferred_element_type=jnp.float32
    ) + jnp.einsum("lmd,cd->lmc", imag_part, mixing[1], preferred_element_type=jnp.float32)
    back_imag = jnp.einsum(
        "lmd,cd->lmc", imag_part, mixing[0], preferred_element_type=jnp.float32
    ) - jnp.einsum("lmd,cd->lmc", real_part, mixing[1], preferred_element_type=jnp.float32)
    coefficient_adjoint = jnp.stack([back_real, back_imag], axis=2).astype(jnp.bfloat16)
    spectrum_adjoint = jnp.einsum(
        "mla,lmrc->amrc", forward, coefficient_adjoint, preferred_element_type=jnp.float32
    ).astype(jnp.bfloat16)
    return spectrum_adjoint.reshape(lat_count, columns, channels)


def to_modes(values):
    return lax.all_to_all(values, ("sec", "tile"), split_axis=1, concat_axis=0, tiled=True)


def to_bands(values):
    return lax.all_to_all(values, ("sec", "tile"), split_axis=0, concat_axis=1, tiled=True)


def rims(values, width):
    with_rows = with_halo(values, (("tile", 0),), width, False)
    return with_halo(with_rows, (("sec", 1),), width, True)


def spread_rows(matrix, values):
    return lax.psum_scatter(
        jnp.dot(matrix, values, precision=lax.Precision.HIGHEST),
        ("sec", "tile"),
        scatter_dimension=0,
        tiled=True,
    )


def collect_rows(matrix, values, lon_count, fields, offset, half):
    piece = lax.all_gather(values, ("sec", "tile"), axis=0, tiled=True)
    own = lax.dynamic_slice_in_dim(
        piece.reshape(piece.shape[0], lon_count, fields), offset, half, 1
    )
    return jnp.dot(
        matrix, own.reshape(piece.shape[0], half * fields), precision=lax.Precision.HIGHEST
    )


def place_half(values, lon_count, offset):
    shape = (values.shape[0], lon_count) + values.shape[2:]
    empty = jnp.zeros(shape, jnp.float32)
    starts = (jnp.int32(0), offset) + tuple((jnp.int32(0) for extra in values.shape[2:]))
    return lax.dynamic_update_slice(empty, values, starts)


def per_device(
    atmosphere,
    ocean_state,
    land_mask,
    crossing_bands,
    ocean_regrid,
    atmosphere_regrid,
    surface_read,
    surface_embed,
    flux_read,
    flux_embed,
    legendre_forward,
    legendre_inverse,
    spectral_mix,
    conv_kernel,
    norm_gain,
    expand_weight,
    project_weight,
    atmosphere_cotangent,
    ocean_cotangent,
):
    band_total = lax.axis_size(("sec", "tile"))
    lat_rows, lon_count, channels = atmosphere.shape
    lat_count = lat_rows * band_total
    ocean_rows, ocean_lon, ocean_channels = ocean_state.shape
    half = lon_count // lax.axis_size("sec")
    offset = lax.axis_index("sec") * half
    ratio = ocean_lon // half
    flux_count = flux_read.shape[1]
    radius = conv_kernel.shape[1] // 2
    layer_count = conv_kernel.shape[0]
    highest = lax.Precision.HIGHEST
    mask_value = land_mask.astype(jnp.float32)
    to_ocean = ocean_matrix(crossing_bands[0], ocean_regrid[0], lat_count)
    to_atmosphere = atmosphere_matrix(crossing_bands[0], atmosphere_regrid[0], lat_count)
    surface = jnp.dot(ocean_state, surface_read, preferred_element_type=jnp.float32)
    coarse = jnp.mean((mask_value * surface).reshape(ocean_rows, half, ratio), axis=2)
    surface_atmosphere = spread_rows(to_atmosphere, place_half(coarse, lon_count, offset))
    flux = jnp.einsum("agc,cf->agf", atmosphere, flux_read, preferred_element_type=jnp.float32)
    flux_ocean = collect_rows(
        to_ocean,
        flux.reshape(lat_rows, lon_count * flux_count),
        lon_count,
        flux_count,
        offset,
        half,
    )
    mixed_input = (
        atmosphere.astype(jnp.float32)
        + surface_atmosphere[:, :, None] * surface_embed[None, None, :]
    ).astype(jnp.bfloat16)
    table = wave_table(lon_count, legendre_forward.shape[0] * band_total)
    spectrum = jnp.einsum(
        "gk,agc->akc", table, mixed_input, preferred_element_type=jnp.float32
    ).astype(jnp.bfloat16)
    returned = to_bands(
        spectral_block(to_modes(spectrum), legendre_forward, legendre_inverse, spectral_mix)
    )
    response = jnp.einsum("gk,akc->agc", table, returned, preferred_element_type=jnp.float32)
    atmosphere_next = (mixed_input.astype(jnp.float32) + jax.nn.gelu(response)).astype(jnp.bfloat16)
    forcing_coarse = jnp.einsum(
        "ogf,fc->ogc",
        flux_ocean.reshape(ocean_rows, half, flux_count),
        flux_embed.astype(jnp.float32),
        precision=highest,
    )
    forcing = jnp.broadcast_to(
        forcing_coarse[:, :, None, :], (ocean_rows, half, ratio, ocean_channels)
    ).reshape(ocean_rows, ocean_lon, ocean_channels)
    state = (ocean_state.astype(jnp.float32) + mask_value[:, :, None] * forcing).astype(
        jnp.bfloat16
    )
    windows = []
    for layer in range(layer_count):
        window = rims(state, radius)
        windows.append(window)
        update = cell_forward(
            depthwise(window, conv_kernel[layer]),
            norm_gain[layer],
            expand_weight[layer],
            project_weight[layer],
        )
        state = (state.astype(jnp.float32) + mask_value[:, :, None] * update).astype(jnp.bfloat16)
    cotangent = ocean_cotangent.astype(jnp.float32)
    for layer in range(layer_count - 1, -1, -1):
        hidden = depthwise(windows[layer], conv_kernel[layer])
        hidden_adjoint = cell_backward(
            hidden,
            norm_gain[layer],
            expand_weight[layer],
            project_weight[layer],
            mask_value,
            cotangent,
        )
        cotangent = cotangent + depthwise(
            rims(hidden_adjoint, radius), conv_kernel[layer, ::-1, ::-1]
        )
    forcing_adjoint = (
        (mask_value[:, :, None] * cotangent)
        .reshape(ocean_rows, half, ratio, ocean_channels)
        .sum(axis=2)
    )
    flux_ocean_adjoint = jnp.einsum(
        "ogc,fc->ogf", forcing_adjoint, flux_embed.astype(jnp.float32), precision=highest
    )
    full_adjoint = place_half(flux_ocean_adjoint, lon_count, offset)
    flux_adjoint = spread_rows(to_ocean.T, full_adjoint.reshape(ocean_rows, lon_count * flux_count))
    flux_adjoint = flux_adjoint.reshape(lat_rows, lon_count, flux_count)
    from_flux = jnp.einsum(
        "agf,cf->agc", flux_adjoint, flux_read.astype(jnp.float32), precision=highest
    )
    atmosphere_adjoint = atmosphere_cotangent.astype(jnp.float32)
    _, gelu_back = jax.vjp(jax.nn.gelu, response)
    response_adjoint = gelu_back(atmosphere_adjoint)[0].astype(jnp.bfloat16)
    returned_adjoint = jnp.einsum(
        "gk,agc->akc", table, response_adjoint, preferred_element_type=jnp.float32
    ).astype(jnp.bfloat16)
    spectrum_adjoint = to_bands(
        spectral_adjoint(
            to_modes(returned_adjoint), legendre_forward, legendre_inverse, spectral_mix
        )
    )
    input_adjoint = atmosphere_adjoint + jnp.einsum(
        "gk,akc->agc", table, spectrum_adjoint, preferred_element_type=jnp.float32
    )
    atmosphere_grad = input_adjoint + from_flux
    surface_adjoint = jnp.einsum("agc,c->ag", input_adjoint, surface_embed, precision=highest)
    coarse_adjoint = collect_rows(to_atmosphere.T, surface_adjoint, lon_count, 1, offset, half)
    widened_adjoint = jnp.broadcast_to(
        coarse_adjoint[:, :, None], (ocean_rows, half, ratio)
    ).reshape(ocean_rows, ocean_lon)
    surface_grad = mask_value * widened_adjoint / ratio
    ocean_grad = (
        cotangent + surface_grad[:, :, None] * surface_read.astype(jnp.float32)[None, None, :]
    )
    return (atmosphere_next, state, atmosphere_grad, ocean_grad)


def solution(mesh):
    return jax.shard_map(
        per_device,
        mesh=mesh,
        in_specs=(
            P(("sec", "tile"), None, None),
            P("tile", "sec", None),
            P("tile", "sec"),
            P("tile", None),
            P("tile", None, None, None),
            P("tile", None, None, None),
            P(),
            P(),
            P(),
            P(),
            P(("sec", "tile"), None, None),
            P(("sec", "tile"), None, None),
            P(),
            P(),
            P(),
            P(),
            P(),
            P(("sec", "tile"), None, None),
            P("tile", "sec", None),
        ),
        out_specs=(
            P(("sec", "tile"), None, None),
            P("tile", "sec", None),
            P(("sec", "tile"), None, None),
            P("tile", "sec", None),
        ),
        check_vma=False,
    )
```

profile of v0, /device:TPU:0, one launch (start us, length us, event | category | flops | bytes accessed | tf_op | source)
XLA Modules:
  0.0 674.6 jit_solution(18413233961991247146)
XLA Ops:
  8.6 44.3 %all-gather.1 = f32[32,1,2880]{2,1,0:T(1,128)S(1)} all-gather(f32[1,1,2880]{2,1,0:T(1,128)S(1)} %reshape.391), channel_id=1, replica_groups=mesh['sec'=2,'tile'=16] {'sec','tile'}, dimensions={0}, use_global_device_ids=true | all-gather | bytes 380160 | tf_op jit(solution)/shard_map/all_gather | solution.py:165
  59.6 2.4 collective-permute-start
  66.6 39.4 %all-reduce.2 = f32[32,360]{1,0:T(8,128)} all-reduce(f32[32,360]{1,0:T(8,128)S(1)} %fusion.381), channel_id=3, replica_groups=mesh['sec'=2,'tile'=16] {'sec','tile'}, use_global_device_ids=true, to_apply=%region_1.0.clone | all-reduce | flops 11520 | bytes 92160
  115.0 3.4 reduce.10
  120.1 5.8 all-to-all-start
  137.1 2.8 bitcast_reduce_fusion.1
  146.7 5.2 all-to-all-start.1
  154.7 21.1 %fusion.368 = (f32[8,720]{1,0:T(8,128)S(1)}, f32[8,720,128]{2,1,0:T(8,128)S(1)}) fusion(f32[128]{0:T(128)S(1)} %get-tuple-element.182, f32[14,726,128]{2,1,0:T(8,128)S(1)} %maximum_convert_fusion, f32[128]{0:T(128)S(1)} %get-tuple-element.183, f32[128]{0:T(128)S(1)} %get-tuple-element.184, f32[128]{0:T(128)S(1)} %get-tuple-element.185, ...), kind=kLoop, calls=%fused_computation.836 | loop fusion | flops 72247680 | bytes 147504128 | tf_op jit(solution)/shard_map/reduce_sum | solution.py:50
  179.5 4.9 add_convert_fusion.1
  194.2 2.4 add_convert_fusion.3
  203.2 3.4 reduce.11
  208.3 11.2 %all-to-all-start.2 = ((bf16[32,2,1536]{2,1,0:T(2,128)(2,1)}), bf16[32,2,1536]{2,1,0:T(2,128)(2,1)}, u32[]{:S(2)}, u32[]{:S(2)}) async-start(bf16[32,2,1536]{2,1,0:T(2,128)(2,1)} %reshape.420), calls=%async_computation.2 | async-start | bytes 393216 | tf_op jit(solution)/shard_map/all_to_all | solution.py:143
  219.9 3.1 maximum_convert_fusion.1
  223.4 20.9 %fusion.366 = (f32[8,720]{1,0:T(8,128)S(1)}, f32[8,720,128]{2,1,0:T(8,128)S(1)}) fusion(f32[128]{0:T(128)S(1)} %copy-done.80, f32[14,726,128]{2,1,0:T(8,128)S(1)} %maximum_convert_fusion.1, f32[128]{0:T(128)S(1)} %copy-done.81, f32[128]{0:T(128)S(1)} %copy-done.82, f32[128]{0:T(128)S(1)} %copy-done.83, f32[128]{0:T(128)S(1)} %copy-done.84, ...), kind=kLoop, calls=%fused_computation.835 | loop fusion | flops 72247680 | bytes 147504128 | tf_op jit(solution)/shard_map/reduce_sum | solution.py:50
  246.2 5.4 fusion.219
  251.6 15.4 %multiply_reduce_fusion.5 = (f32[8,720]{1,0:T(8,128)S(1)}, f32[8,720]{1,0:T(8,128)S(1)}, f32[8,720,128]{2,1,0:T(8,128)}) fusion(f32[128]{0:T(128)S(1)} %copy-done.43, f32[8,720]{1,0:T(8,128)S(1)} %add_rsqrt_fusion, f32[8,720,128]{2,1,0:T(8,128)} %copy-done.2, f32[8,720]{1,0:T(8,128)S(1)} %broadcast_multiply_fusion.6, ...), kind=kOutput, calls=%fused_computation.438 | convolution fusion | flops 1575555840 | bytes 19551744 | tf_op jit(solution)/shard_map/dot_general | solution.py:68
  267.1 6.8 %multiply_convert_fusion.6 = bf16[8,720,128]{2,1,0:T(8,128)(2,1)S(1)} fusion(f32[8,720,128]{2,1,0:T(8,128)} %get-tuple-element.236, f32[8,720,128]{2,1,0:T(8,128)} %copy-done.2, f32[8,720]{1,0:T(8,128)S(1)} %broadcast_multiply_fusion.4, f32[8,720]{1,0:T(8,128)S(1)} %broadcast_multiply_fusion.5, f32[128]{0:T(128)S(1)} %copy-done.43, ...), kind=kLoop, calls=%fused_computation.422 | loop fusion | flops 5898240 | bytes 7465472 | tf_op jit(solution)/shard_map/convert_element_type | solution.py:75
  281.9 2.8 bitcast_reduce_fusion
  296.9 8.0 %all-to-all-start.3 = ((bf16[32,8,384]{2,1,0:T(8,128)(2,1)}), bf16[32,8,384]{2,1,0:T(8,128)(2,1)}, u32[]{:S(2)}, u32[]{:S(2)}) async-start(bf16[32,8,384]{2,1,0:T(8,128)(2,1)} %copy.86), calls=%async_computation.3 | async-start | bytes 393216 | tf_op jit(solution)/shard_map/all_to_all | solution.py:147
  305.3 4.9 maximum_convert_fusion.2
  310.5 62.1 %convert_add_fusion = f32[8,720,128]{2,1,0:T(8,128)} fusion(bf16[8,720,128]{2,1,0:T(8,128)(2,1)S(1)} %copy-done.15, f32[14,726,128]{2,1,0:T(8,128)} %maximum_convert_fusion.2, f32[128]{0:T(128)S(1)} %copy-done.53, f32[128]{0:T(128)S(1)} %copy-done.54, f32[128]{0:T(128)S(1)} %copy-done.55, f32[128]{0:T(128)S(1)} %copy-done.56, f32[128]{0:T(128)S(1)} %copy-done.57, ...), kind=kLoop, calls=%fused_computation.26 | loop fusion | flops 72990720 | bytes 148955648 | tf_op jit(solution)/shard_map/add | solution.py:275
  372.6 13.5 %multiply_reduce_fusion.4 = (f32[8,720]{1,0:T(8,128)S(1)}, f32[8,720]{1,0:T(8,128)S(1)}, f32[8,720,128]{2,1,0:T(8,128)}) fusion(f32[128]{0:T(128)S(1)} %get-tuple-element.233, f32[8,720]{1,0:T(8,128)S(1)} %copy-done.31, f32[8,720,128]{2,1,0:T(8,128)S(1)} %get-tuple-element.15, f32[8,720]{1,0:T(8,128)S(1)} %copy-done.19, ...), kind=kOutput, calls=%fused_computation.437 | convolution fusion | flops 1574818560 | bytes 21026304 | tf_op jit(solution)/shard_map/dot_general | solution.py:68
  386.1 7.0 %multiply_convert_fusion.4 = bf16[8,720,128]{2,1,0:T(8,128)(2,1)S(1)} fusion(f32[8,720,128]{2,1,0:T(8,128)} %get-tuple-element.237, f32[8,720,128]{2,1,0:T(8,128)S(1)} %get-tuple-element.15, f32[8,720]{1,0:T(8,128)S(1)} %broadcast_multiply_fusion.2, f32[8,720]{1,0:T(8,128)S(1)} %broadcast_multiply_fusion.3, f32[128]{0:T(128)S(1)} %get-tuple-element.233, ...), kind=kLoop, calls=%fused_computation.419 | loop fusion | flops 5898240 | bytes 7465472 | tf_op jit(solution)/shard_map/convert_element_type | solution.py:75
  395.3 2.2 collective-permute-start.12
  401.6 46.3 %all-reduce.1 = f32[32,360]{1,0:T(8,128)S(1)} all-reduce(f32[32,360]{1,0:T(8,128)S(1)} %reshape.388), channel_id=2, replica_groups=mesh['sec'=2,'tile'=16] {'sec','tile'}, use_global_device_ids=true, to_apply=%add | all-reduce | flops 11520 | bytes 92160
  449.2 2.3 collective-permute-start.14
  455.2 3.4 maximum_convert_fusion.3
  458.7 61.6 %multiply_add_fusion = (f32[8,720,128]{2,1,0:T(8,128)}, f32[8,720,128]{2,1,0:T(8,128)S(1)}) fusion(f32[128]{0:T(128)} %convert_element_type.259, f32[8,720]{1,0:T(8,128)} %multiply_multiply_fusion.6, f32[8,720,128]{2,1,0:T(8,128)} %convert_add_fusion, f32[128]{0:T(128)S(1)} %copy-done.45, f32[14,726,128]{2,1,0:T(8,128)} %maximum_convert_fusion.3, ...), kind=kLoop, calls=%fused_computation.418 | loop fusion | flops 73728000 | bytes 153402880 | tf_op jit(solution)/shard_map/add | solution.py:314
  522.4 3.6 reduce_sum.115
  527.5 8.5 %dynamic_update_slice.7 = f32[8,360,8]{2,1,0:T(8,128)S(1)} dynamic-update-slice(f32[8,360,8]{2,1,0:T(8,128)S(1)} %broadcast_in_dim.10, f32[8,180,8]{2,1,0:T(8,128)} %fusion.326, s32[]{:T(128)} %constant.23.clone.1, s32[]{:T(128)S(6)} %select_n.26, s32[]{:T(128)} %constant.23.clone.1) | dynamic-update-slice | bytes 92164 | tf_op jit(solution)/shard_map/dynamic_update_slice | solution.py:178
  539.2 8.3 %add_convert_fusion = bf16[8,720,128]{2,1,0:T(8,128)(2,1)} fusion(bf16[8,720,128]{2,1,0:T(8,128)(2,1)S(1)} %copy-done.12, f32[8,720,512]{2,1,0:T(8,128)} %fusion.219, f32[8,720]{1,0:T(8,128)} %copy-done.24, bf16[2,512,128]{2,1,0:T(8,128)(2,1)} %param.35), kind=kOutput, calls=%fused_computation.424 | convolution fusion | flops 784465920 | bytes 14901248 | tf_op jit(solution)/shard_map/dot_general | solution.py:55
  547.5 117.5 %all-reduce.6.cloned.1.call-done = f32[32,2880]{1,0:T(8,128)} async-done(((f32[32,2880]{1,0:T(8,128)}), f32[32,2880]{1,0:T(8,128)}) %all-reduce.6.cloned.1.call-update) | async-done | bytes 368656
  (472 shorter events, 107.1 us)
Async XLA Ops:
  7.2 138.6 %copy-start = (bf16[4,32,32]{2,1,0:T(8,128)(2,1)S(1)}, bf16[4,32,32]{2,1,0:T(8,128)(2,1)}, u32[]{:S(2)}) copy-start(bf16[4,32,32]{2,1,0:T(8,128)(2,1)} %param.30) | copy-start | bytes 24580
  54.6 124.9 %copy-start.24 = (f32[8,720]{1,0:T(8,128)}, f32[8,720]{1,0:T(8,128)S(1)}, u32[]{:S(2)}) copy-start(f32[8,720]{1,0:T(8,128)S(1)} %convert_element_type.207) | copy-start | bytes 69124
  58.5 93.8 %copy-start.3 = (bf16[8,720,128]{2,1,0:T(8,128)(2,1)}, bf16[8,720,128]{2,1,0:T(8,128)(2,1)S(1)}, u32[]{:S(2)}) copy-start(bf16[8,720,128]{2,1,0:T(8,128)(2,1)S(1)} %add_convert_fusion.2) | copy-start | bytes 4423684
  59.6 84.0 %collective-permute-start = (bf16[3,720,128]{2,1,0:T(8,128)(2,1)}, bf16[3,720,128]{2,1,0:T(8,128)(2,1)S(1)}, u32[]{:S(2)}, u32[]{:S(2)}) collective-permute-start(bf16[3,720,128]{2,1,0:T(8,128)(2,1)} %get-tuple-element.32), channel_id=1, source_target_pairs={{0,1},{1,2},{2,3},{3,4},{4,5},{5,6},{6,7},{7,8},{8,9},{9,10},{10,1... | collective-permute-start | bytes 1658888 | tf_op jit(solution)/shard_map/ppermute | solution.py:14
  62.0 81.6 %collective-permute-start.1 = (bf16[3,720,128]{2,1,0:T(8,128)(2,1)}, bf16[3,720,128]{2,1,0:T(8,128)(2,1)S(1)}, u32[]{:S(2)}, u32[]{:S(2)}) collective-permute-start(bf16[3,720,128]{2,1,0:T(8,128)(2,1)} %get-tuple-element.33), channel_id=1, source_target_pairs={{1,0},{2,1},{3,2},{4,3},{5,4},{6,5},{7,6},{8,7},{9,8},{10,9},{11,1... | collective-permute-start | bytes 1658888 | tf_op jit(solution)/shard_map/ppermute | solution.py:15
  64.8 61.1 %copy-start.33 = (bf16[2,7,7,128]{3,0,2,1:T(2,128)(2,1)S(1)}, bf16[2,7,7,128]{3,0,2,1:T(2,128)(2,1)}, u32[]{:S(2)}) copy-start(bf16[2,7,7,128]{3,0,2,1:T(2,128)(2,1)} %param.32) | copy-start | bytes 75268
  120.1 14.7 %all-to-all-start = ((bf16[32,2,1536]{2,1,0:T(2,128)(2,1)}), bf16[32,2,1536]{2,1,0:T(2,128)(2,1)}, u32[]{:S(2)}, u32[]{:S(2)}) async-start(bf16[32,2,1536]{2,1,0:T(2,128)(2,1)} %reshape.418), calls=%async_computation | async-start | bytes 393216 | tf_op jit(solution)/shard_map/all_to_all | solution.py:143
  143.7 8.6 %collective-permute-start.2 = (bf16[14,3,128]{2,1,0:T(4,128)(2,1)S(1)}, bf16[14,3,128]{2,1,0:T(4,128)(2,1)S(1)}, u32[]{:S(2)}, u32[]{:S(2)}) collective-permute-start(bf16[14,3,128]{2,1,0:T(4,128)(2,1)S(1)} %get-tuple-element.24), channel_id=1, source_target_pairs={{0,16},{16,0},{1,17},{17,1},{2,18},{18,2},{3,19},{19,3},{4,20},{20... | collective-permute-start | bytes 32264 | tf_op jit(solution)/shard_map/ppermute | solution.py:14
  144.7 7.6 %collective-permute-start.3 = (bf16[14,3,128]{2,1,0:T(4,128)(2,1)S(1)}, bf16[14,3,128]{2,1,0:T(4,128)(2,1)S(1)}, u32[]{:S(2)}, u32[]{:S(2)}) collective-permute-start(bf16[14,3,128]{2,1,0:T(4,128)(2,1)S(1)} %get-tuple-element.25), channel_id=1, source_target_pairs={{16,0},{0,16},{17,1},{1,17},{18,2},{2,18},{19,3},{3,19},{20,4},{4,... | collective-permute-start | bytes 32264 | tf_op jit(solution)/shard_map/ppermute | solution.py:15
  146.7 47.5 %all-to-all-start.1 = ((bf16[32,8,384]{2,1,0:T(8,128)(2,1)}), bf16[32,8,384]{2,1,0:T(8,128)(2,1)}, u32[]{:S(2)}, u32[]{:S(2)}) async-start(bf16[32,8,384]{2,1,0:T(8,128)(2,1)} %copy.74), calls=%async_computation.1 | async-start | bytes 393216 | tf_op jit(solution)/shard_map/all_to_all | solution.py:147
  186.0 10.7 %collective-permute-start.4 = (bf16[3,720,128]{2,1,0:T(8,128)(2,1)}, bf16[3,720,128]{2,1,0:T(8,128)(2,1)S(1)}, u32[]{:S(2)}, u32[]{:S(2)}) collective-permute-start(bf16[3,720,128]{2,1,0:T(8,128)(2,1)} %get-tuple-element.30), channel_id=1, source_target_pairs={{0,1},{1,2},{2,3},{3,4},{4,5},{5,6},{6,7},{7,8},{8,9},{9,10},{10,1... | collective-permute-start | bytes 1658888 | tf_op jit(solution)/shard_map/ppermute | solution.py:14
  188.1 8.6 %collective-permute-start.5 = (bf16[3,720,128]{2,1,0:T(8,128)(2,1)}, bf16[3,720,128]{2,1,0:T(8,128)(2,1)}, u32[]{:S(2)}, u32[]{:S(2)}) collective-permute-start(bf16[3,720,128]{2,1,0:T(8,128)(2,1)} %get-tuple-element.31), channel_id=1, source_target_pairs={{1,0},{2,1},{3,2},{4,3},{5,4},{6,5},{7,6},{8,7},{9,8},{10,9},{11,1... | collective-permute-start | bytes 1658888 | tf_op jit(solution)/shard_map/ppermute | solution.py:15
  198.0 21.9 %collective-permute-start.6 = (bf16[14,3,128]{2,1,0:T(4,128)(2,1)}, bf16[14,3,128]{2,1,0:T(4,128)(2,1)S(1)}, u32[]{:S(2)}, u32[]{:S(2)}) collective-permute-start(bf16[14,3,128]{2,1,0:T(4,128)(2,1)} %get-tuple-element.22), channel_id=1, source_target_pairs={{0,16},{16,0},{1,17},{17,1},{2,18},{18,2},{3,19},{19,3},{4,20},{20... | collective-permute-start | bytes 32264 | tf_op jit(solution)/shard_map/ppermute | solution.py:14
  199.6 20.3 %collective-permute-start.7 = (bf16[14,3,128]{2,1,0:T(4,128)(2,1)}, bf16[14,3,128]{2,1,0:T(4,128)(2,1)}, u32[]{:S(2)}, u32[]{:S(2)}) collective-permute-start(bf16[14,3,128]{2,1,0:T(4,128)(2,1)} %get-tuple-element.23), channel_id=1, source_target_pairs={{16,0},{0,16},{17,1},{1,17},{18,2},{2,18},{19,3},{3,19},{20,4},{4,... | collective-permute-start | bytes 32264 | tf_op jit(solution)/shard_map/ppermute | solution.py:15
  208.3 71.4 %all-to-all-start.2 = ((bf16[32,2,1536]{2,1,0:T(2,128)(2,1)}), bf16[32,2,1536]{2,1,0:T(2,128)(2,1)}, u32[]{:S(2)}, u32[]{:S(2)}) async-start(bf16[32,2,1536]{2,1,0:T(2,128)(2,1)} %reshape.420), calls=%async_computation.2 | async-start | bytes 393216 | tf_op jit(solution)/shard_map/all_to_all | solution.py:143
  276.1 16.5 %collective-permute-start.8 = (bf16[3,720,128]{2,1,0:T(8,128)(2,1)}, bf16[3,720,128]{2,1,0:T(8,128)(2,1)S(1)}, u32[]{:S(2)}, u32[]{:S(2)}) collective-permute-start(bf16[3,720,128]{2,1,0:T(8,128)(2,1)} %get-tuple-element.28), channel_id=1, source_target_pairs={{0,1},{1,2},{2,3},{3,4},{4,5},{5,6},{6,7},{7,8},{8,9},{9,10},{10,1... | collective-permute-start | bytes 1658888 | tf_op jit(solution)/shard_map/ppermute | solution.py:14
  278.2 14.4 %collective-permute-start.9 = (bf16[3,720,128]{2,1,0:T(8,128)(2,1)}, bf16[3,720,128]{2,1,0:T(8,128)(2,1)}, u32[]{:S(2)}, u32[]{:S(2)}) collective-permute-start(bf16[3,720,128]{2,1,0:T(8,128)(2,1)} %get-tuple-element.29), channel_id=1, source_target_pairs={{1,0},{2,1},{3,2},{4,3},{5,4},{6,5},{7,6},{8,7},{9,8},{10,9},{11,1... | collective-permute-start | bytes 1658888 | tf_op jit(solution)/shard_map/ppermute | solution.py:15
  293.9 11.4 %collective-permute-start.10 = (bf16[14,3,128]{2,1,0:T(4,128)(2,1)}, bf16[14,3,128]{2,1,0:T(4,128)(2,1)S(1)}, u32[]{:S(2)}, u32[]{:S(2)}) collective-permute-start(bf16[14,3,128]{2,1,0:T(4,128)(2,1)} %get-tuple-element.20), channel_id=1, source_target_pairs={{0,16},{16,0},{1,17},{17,1},{2,18},{18,2},{3,19},{19,3},{4,20},{20... | collective-permute-start | bytes 32264 | tf_op jit(solution)/shard_map/ppermute | solution.py:14
  295.5 9.8 %collective-permute-start.11 = (bf16[14,3,128]{2,1,0:T(4,128)(2,1)S(1)}, bf16[14,3,128]{2,1,0:T(4,128)(2,1)S(1)}, u32[]{:S(2)}, u32[]{:S(2)}) collective-permute-start(bf16[14,3,128]{2,1,0:T(4,128)(2,1)S(1)} %get-tuple-element.21), channel_id=1, source_target_pairs={{16,0},{0,16},{17,1},{1,17},{18,2},{2,18},{19,3},{3,19},{20,4},{4,... | collective-permute-start | bytes 32264 | tf_op jit(solution)/shard_map/ppermute | solution.py:15
  296.9 102.2 %all-to-all-start.3 = ((bf16[32,8,384]{2,1,0:T(8,128)(2,1)}), bf16[32,8,384]{2,1,0:T(8,128)(2,1)}, u32[]{:S(2)}, u32[]{:S(2)}) async-start(bf16[32,8,384]{2,1,0:T(8,128)(2,1)} %copy.86), calls=%async_computation.3 | async-start | bytes 393216 | tf_op jit(solution)/shard_map/all_to_all | solution.py:147
  305.0 360.0 %all-reduce.6.cloned.1.call-start = ((), (), s32[]{:S(2)}) async-start(), calls=%async_computation.4 | async-start | bytes 753664
  310.4 62.1 %copy-start.19 = (f32[8,720]{1,0:T(8,128)S(1)}, f32[8,720]{1,0:T(8,128)}, u32[]{:S(2)}) copy-start(f32[8,720]{1,0:T(8,128)} %copy-done.18) | copy-start | bytes 69124
  310.4 62.1 %copy-start.23 = (bf16[2,128,512]{2,1,0:T(8,128)(2,1)S(1)}, bf16[2,128,512]{2,1,0:T(8,128)(2,1)}, u32[]{:S(2)}) copy-start(bf16[2,128,512]{2,1,0:T(8,128)(2,1)} %param.34) | copy-start | bytes 786436
  310.5 62.1 %copy-start.26 = (f32[8,720]{1,0:T(8,128)S(1)}, f32[8,720]{1,0:T(8,128)}, u32[]{:S(2)}) copy-start(f32[8,720]{1,0:T(8,128)} %copy-done.24) | copy-start | bytes 69124
  310.5 62.1 %copy-start.31 = (f32[8,720]{1,0:T(8,128)S(1)}, f32[8,720]{1,0:T(8,128)}, u32[]{:S(2)}) copy-start(f32[8,720]{1,0:T(8,128)} %copy-done.30) | copy-start | bytes 69124
  395.3 53.9 %collective-permute-start.12 = (bf16[3,720,128]{2,1,0:T(8,128)(2,1)}, bf16[3,720,128]{2,1,0:T(8,128)(2,1)S(1)}, u32[]{:S(2)}, u32[]{:S(2)}) collective-permute-start(bf16[3,720,128]{2,1,0:T(8,128)(2,1)} %get-tuple-element.26), channel_id=1, source_target_pairs={{0,1},{1,2},{2,3},{3,4},{4,5},{5,6},{6,7},{7,8},{8,9},{9,10},{10,1... | collective-permute-start | bytes 1658888 | tf_op jit(solution)/shard_map/ppermute | solution.py:14
  397.6 51.6 %collective-permute-start.13 = (bf16[3,720,128]{2,1,0:T(8,128)(2,1)}, bf16[3,720,128]{2,1,0:T(8,128)(2,1)S(1)}, u32[]{:S(2)}, u32[]{:S(2)}) collective-permute-start(bf16[3,720,128]{2,1,0:T(8,128)(2,1)} %get-tuple-element.27), channel_id=1, source_target_pairs={{1,0},{2,1},{3,2},{4,3},{5,4},{6,5},{7,6},{8,7},{9,8},{10,9},{11,1... | collective-permute-start | bytes 1658888 | tf_op jit(solution)/shard_map/ppermute | solution.py:15
  449.2 4.0 collective-permute-start.14
  451.5 3.7 collective-permute-start.15
  458.7 61.6 %copy-start.27 = (f32[8,720]{1,0:T(8,128)S(1)}, f32[8,720]{1,0:T(8,128)}, u32[]{:S(2)}) copy-start(f32[8,720]{1,0:T(8,128)} %copy-done.24) | copy-start | bytes 69124
  539.2 126.8 %copy-start.35 = (bf16[384,8]{0,1:T(8,128)(2,1)S(1)}, bf16[384,8]{0,1:T(8,128)(2,1)}, u32[]{:S(2)}) copy-start(bf16[384,8]{0,1:T(8,128)(2,1)} %param.27) | copy-start | bytes 18436
  539.2 128.1 %copy-start.1 = (bf16[4,32,32]{2,1,0:T(8,128)(2,1)S(1)}, bf16[4,32,32]{2,1,0:T(8,128)(2,1)}, u32[]{:S(2)}) copy-start(bf16[4,32,32]{2,1,0:T(8,128)(2,1)} %param.30) | copy-start | bytes 24580
  (154 other events, 1028.8 us)
Sparse Core Ops, SparseCore 0:
  539.3 125.6 all-reduce.5
where the time goes:
time: 683 us; the launch traced here: 675 us
  other arithmetic  217 us (32%)
  blocking collectives  130 us (19%)
  waiting for transfers between devices  121 us (18%)
  matrix products  75.4 us (11%)
  local copies, waits for them, and re-layouts  60.2 us (9%)
  starting transfers between devices  53.5 us (8%)
  between operations  17.5 us (3%)
    unnamed x2, waiting for transfers between devices  118 us
    unnamed x2, blocking collectives  85.8 us
    add x1, other arithmetic, per_device(): cotangent + depthwise(rims(hidden_adjoint, radius), conv_kernel[layer, ::...  62.1 us
    add x1, other arithmetic, per_device(): cotangent + surface_grad[:, :, None] * surface_read.astype(jnp.float32)[N...  61.6 us
    all_gather x1, blocking collectives, collect_rows(): piece = lax.all_gather(values, ('sec', 'tile'), axis=0, tiled=True)  44.3 us
    reduce_sum x2, other arithmetic, cell_forward(): center = hidden - jnp.mean(hidden, axis=-1, keepdims=True)  42 us
    dot_general x2, matrix products, cell_backward(): jnp.dot(before_adjoint, expand.T, preferred_element_type=jnp.float32)  29 us
    all_to_all x2, starting transfers between devices, to_modes(): lax.all_to_all(values, ('sec', 'tile'), split_axis=1, concat_axis=0, tile...  16.9 us
  transfers between devices with their start and end apart: 21, of which 4 were waited for; matrix products, arithmetic and copies ran while one was open for 37% of the time, Pallas kernels for 0%

commit v1 on v0

--- a/solution.py
+++ b/solution.py
@@ -1,6 +1,8 @@
 import jax
 import jax.numpy as jnp
 from jax import lax
+from jax.experimental import pallas as pl
+from jax.experimental.pallas import tpu as pltpu
 from jax.sharding import PartitionSpec as P
 
 
@@ -29,50 +31,148 @@
     return scaled.reshape(lon_count, 2 * mode_count).astype(jnp.bfloat16)
 
 
-def depthwise(window, kernel):
-    radius = kernel.shape[0] // 2
-    height = window.shape[0] - 2 * radius
-    extent = window.shape[1] - 2 * radius
-    wide = window.astype(jnp.float32)
-    weights = kernel.astype(jnp.float32)
-    total = jnp.zeros((height, extent, window.shape[2]), jnp.float32)
-    for shift_row in range(kernel.shape[0]):
-        for shift_col in range(kernel.shape[1]):
-            total = (
-                total
-                + wide[shift_row : shift_row + height, shift_col : shift_col + extent]
-                * weights[shift_row, shift_col]
-            )
-    return total
-
-
-def cell_forward(hidden, gain, expand, project):
-    center = hidden - jnp.mean(hidden, axis=-1, keepdims=True)
-    inverse_std = lax.rsqrt(jnp.mean(center * center, axis=-1, keepdims=True) + 1e-06)
-    normed = (center * inverse_std * gain).astype(jnp.bfloat16)
-    before = jnp.dot(normed, expand, preferred_element_type=jnp.float32)
-    active = jax.nn.gelu(before).astype(jnp.bfloat16)
-    return jnp.dot(active, project, preferred_element_type=jnp.float32)
-
-
-def cell_backward(hidden, gain, expand, project, mask_value, cotangent):
+GELU_SCALE = 0.7978845608028654
+GELU_CUBIC = 0.044715
+
+
+def conv_into(window, taps, store, side):
+    rows = window.shape[0] - side + 1
+    extent = window.shape[1] - side + 1
+
+    def step(index, carry):
+        start = pl.multiple_of(index * 8, 8)
+        totals = [None] * rows
+        for col in range(side):
+            weights = [taps[row * side + col] for row in range(side)]
+            for line in range(rows + side - 1):
+                piece = window[line, pl.ds(start + col, 8), :]
+                for row in range(side):
+                    target = line - row
+                    if 0 <= target < rows:
+                        term = piece * weights[row]
+                        totals[target] = term if totals[target] is None else totals[target] + term
+        for row in range(rows):
+            store(row, start, totals[row])
+        return carry
+
+    lax.fori_loop(0, extent // 8, step, jnp.int32(0))
+
+
+def widen(narrow, wide):
+    def step(line, carry):
+        wide[line] = narrow[line].astype(jnp.float32)
+        return carry
+
+    lax.fori_loop(0, narrow.shape[0], step, jnp.int32(0))
+
+
+def forward_kernel(
+    narrow, taps, mask, gain, expand, project, state_out, hidden_out, window
+):
+    widen(narrow, window)
+    rows, extent, _ = state_out.shape
+    side = window.shape[0] - rows + 1
+    radius = side // 2
+
+    def store(row, start, value):
+        hidden_out[row, pl.ds(start, 8), :] = value
+
+    conv_into(window, taps, store, side)
+
+    def cells(row, carry):
+        hidden = hidden_out[row]
+        center = hidden - jnp.mean(hidden, axis=-1, keepdims=True)
+        inverse_std = lax.rsqrt(jnp.mean(center * center, axis=-1, keepdims=True) + 1e-06)
+        normed = (center * inverse_std * gain[...]).astype(jnp.bfloat16)
+        before = jnp.dot(normed, expand[...], preferred_element_type=jnp.float32)
+        inner = before * (GELU_SCALE + (GELU_SCALE * GELU_CUBIC) * (before * before))
+        scaled = 0.5 * before
+        active = (scaled + scaled * jnp.tanh(inner)).astype(jnp.bfloat16)
+        update = jnp.dot(active, project[...], preferred_element_type=jnp.float32)
+        old = window[row + radius, radius : radius + extent, :]
+        state_out[row] = (old + mask[row].astype(jnp.float32) * update).astype(jnp.bfloat16)
+        return carry
+
+    lax.fori_loop(0, rows, cells, jnp.int32(0))
+
+
+def cell_backward(hidden, cotangent, mask, gain, expand, expand_t, project_t):
     center = hidden - jnp.mean(hidden, axis=-1, keepdims=True)
     inverse_std = lax.rsqrt(jnp.mean(center * center, axis=-1, keepdims=True) + 1e-06)
     unit = center * inverse_std
     normed = (unit * gain).astype(jnp.bfloat16)
     before = jnp.dot(normed, expand, preferred_element_type=jnp.float32)
-    masked = (mask_value[:, :, None] * cotangent).astype(jnp.bfloat16)
-    active_adjoint = jnp.dot(masked, project.T, preferred_element_type=jnp.float32)
-    _, gelu_back = jax.vjp(jax.nn.gelu, before)
-    before_adjoint = gelu_back(active_adjoint)[0].astype(jnp.bfloat16)
-    normed_adjoint = jnp.dot(before_adjoint, expand.T, preferred_element_type=jnp.float32)
-    scaled = normed_adjoint * gain
-    result = inverse_std * (
-        scaled
-        - jnp.mean(scaled, axis=-1, keepdims=True)
-        - unit * jnp.mean(scaled * unit, axis=-1, keepdims=True)
-    )
-    return result.astype(jnp.bfloat16)
+    masked = (mask.astype(jnp.float32) * cotangent).astype(jnp.bfloat16)
+    active_adjoint = jnp.dot(masked, project_t, preferred_element_type=jnp.float32)
+    square = before * before
+    wave = jnp.tanh(before * (GELU_SCALE + (GELU_SCALE * GELU_CUBIC) * square))
+    slope = (0.5 * GELU_SCALE + (1.5 * GELU_SCALE * GELU_CUBIC) * square) * before
+    derivative = 0.5 + 0.5 * wave + slope * (1.0 - wave * wave)
+    before_adjoint = (derivative * active_adjoint).astype(jnp.bfloat16)
+    scaled = jnp.dot(before_adjoint, expand_t, preferred_element_type=jnp.float32) * gain
+    return (
+        inverse_std
+        * (
+            scaled
+            - jnp.mean(scaled, axis=-1, keepdims=True)
+            - unit * jnp.mean(scaled * unit, axis=-1, keepdims=True)
+        )
+    ).astype(jnp.bfloat16)
+
+
+def backward_kernel(hidden, cotangent, mask, gain, expand, expand_t, project_t, adjoint_out):
+    def cells(row, carry):
+        adjoint_out[row] = cell_backward(
+            hidden[row],
+            cotangent[row].astype(jnp.float32),
+            mask[row],
+            gain[...],
+            expand[...],
+            expand_t[...],
+            project_t[...],
+        )
+        return carry
+
+    lax.fori_loop(0, hidden.shape[0], cells, jnp.int32(0))
+
+
+def adjoint_kernel(narrow, taps, cotangent, cotangent_out, window):
+    widen(narrow, window)
+    side = window.shape[0] - cotangent.shape[0] + 1
+
+    def store(row, start, value):
+        old = cotangent[row, pl.ds(start, 8), :].astype(jnp.float32)
+        cotangent_out[row, pl.ds(start, 8), :] = old + value
+
+    conv_into(window, taps, store, side)
+
+
+def adjoint_backward_kernel(
+    narrow, taps, cotangent, hidden, mask, gain, expand, expand_t, project_t,
+    cotangent_out, adjoint_out, window,
+):
+    adjoint_kernel(narrow, taps, cotangent, cotangent_out, window)
+    backward_kernel(
+        hidden, cotangent_out, mask, gain, expand, expand_t, project_t, adjoint_out
+    )
+
+
+def run_kernel(kernel, outs, flops, *operands, scratch=()):
+    size = sum(x.size * x.dtype.itemsize for x in operands)
+    return pl.pallas_call(
+        kernel,
+        out_shape=outs,
+        in_specs=[pl.BlockSpec(memory_space=pltpu.VMEM)] * len(operands),
+        scratch_shapes=list(scratch),
+        out_specs=jax.tree.map(lambda _: pl.BlockSpec(memory_space=pltpu.VMEM), outs),
+        cost_estimate=pl.CostEstimate(flops=flops, bytes_accessed=size, transcendentals=0),
+    )(*operands)
+
+
+def tap_tiles(kernel):
+    side, _, channels = kernel.shape
+    flat = kernel.astype(jnp.float32).reshape(side * side, 1, channels)
+    return jnp.broadcast_to(flat, (side * side, 8, channels))
 
 
 def ocean_matrix(bands_row, blocks, lat_count):
@@ -152,30 +252,22 @@
     return with_halo(with_rows, (("sec", 1),), width, True)
 
 
-def spread_rows(matrix, values):
-    return lax.psum_scatter(
-        jnp.dot(matrix, values, precision=lax.Precision.HIGHEST),
-        ("sec", "tile"),
-        scatter_dimension=0,
-        tiled=True,
-    )
-
-
-def collect_rows(matrix, values, lon_count, fields, offset, half):
-    piece = lax.all_gather(values, ("sec", "tile"), axis=0, tiled=True)
-    own = lax.dynamic_slice_in_dim(
-        piece.reshape(piece.shape[0], lon_count, fields), offset, half, 1
-    )
-    return jnp.dot(
-        matrix, own.reshape(piece.shape[0], half * fields), precision=lax.Precision.HIGHEST
-    )
-
-
-def place_half(values, lon_count, offset):
-    shape = (values.shape[0], lon_count) + values.shape[2:]
-    empty = jnp.zeros(shape, jnp.float32)
-    starts = (jnp.int32(0), offset) + tuple((jnp.int32(0) for extra in values.shape[2:]))
-    return lax.dynamic_update_slice(empty, values, starts)
+def swap(values):
+    return lax.all_to_all(values, ("sec", "tile"), split_axis=0, concat_axis=0, tiled=True)
+
+
+def for_halves(values, sections):
+    lat_rows = values.shape[0]
+    parts = jnp.moveaxis(values.reshape(lat_rows, sections, -1), 1, 0)
+    tiles = lax.axis_size("tile")
+    spread = jnp.broadcast_to(parts[:, None], (sections, tiles) + parts.shape[1:])
+    return spread.reshape((sections * tiles,) + parts.shape[1:])
+
+
+def sum_halves(received, sections):
+    count, lat_rows, width = received.shape
+    total = received.reshape(sections, count // sections, lat_rows, width).sum(axis=1)
+    return jnp.moveaxis(total, 0, 1).reshape(lat_rows, sections * width)
 
 
 def per_device(
@@ -204,7 +296,6 @@
     lat_count = lat_rows * band_total
     ocean_rows, ocean_lon, ocean_channels = ocean_state.shape
     half = lon_count // lax.axis_size("sec")
-    offset = lax.axis_index("sec") * half
     ratio = ocean_lon // half
     flux_count = flux_read.shape[1]
     radius = conv_kernel.shape[1] // 2
@@ -215,15 +306,22 @@
     to_atmosphere = atmosphere_matrix(crossing_bands[0], atmosphere_regrid[0], lat_count)
     surface = jnp.dot(ocean_state, surface_read, preferred_element_type=jnp.float32)
     coarse = jnp.mean((mask_value * surface).reshape(ocean_rows, half, ratio), axis=2)
-    surface_atmosphere = spread_rows(to_atmosphere, place_half(coarse, lon_count, offset))
+    sections = lax.axis_size("sec")
     flux = jnp.einsum("agc,cf->agf", atmosphere, flux_read, preferred_element_type=jnp.float32)
-    flux_ocean = collect_rows(
-        to_ocean,
-        flux.reshape(lat_rows, lon_count * flux_count),
-        lon_count,
-        flux_count,
-        offset,
-        half,
+    coarse_parts = jnp.dot(to_atmosphere, coarse, precision=highest)
+    arrived = swap(
+        jnp.concatenate(
+            [
+                for_halves(flux.reshape(lat_rows, lon_count * flux_count), sections),
+                coarse_parts.reshape(band_total, lat_rows, half),
+            ],
+            axis=2,
+        )
+    )
+    flux_width = half * flux_count
+    surface_atmosphere = sum_halves(arrived[:, :, flux_width:], sections)
+    flux_ocean = jnp.dot(
+        to_ocean, arrived[:, :, :flux_width].reshape(lat_count, flux_width), precision=highest
     )
     mixed_input = (
         atmosphere.astype(jnp.float32)
@@ -250,31 +348,82 @@
     state = (ocean_state.astype(jnp.float32) + mask_value[:, :, None] * forcing).astype(
         jnp.bfloat16
     )
-    windows = []
+    mask_wide = jnp.broadcast_to(
+        mask_value[:, :, None], (ocean_rows, ocean_lon, ocean_channels)
+    ).astype(jnp.bfloat16)
+    shape = (ocean_rows, ocean_lon, ocean_channels)
+    narrow = jax.ShapeDtypeStruct(shape, jnp.bfloat16)
+    wide = jax.ShapeDtypeStruct(shape, jnp.float32)
+    hidden_units = expand_weight.shape[2]
+    work = ocean_rows * ocean_lon * ocean_channels
+    conv_flops = 2000 * work
+    cell_flops = 8 * work * hidden_units
+    gains = norm_gain[:, None, :]
+    hiddens = []
+    window_scratch = (
+        pltpu.VMEM(
+            (ocean_rows + 2 * radius, ocean_lon + 2 * radius, ocean_channels), jnp.float32
+        ),
+    )
     for layer in range(layer_count):
-        window = rims(state, radius)
-        windows.append(window)
-        update = cell_forward(
-            depthwise(window, conv_kernel[layer]),
-            norm_gain[layer],
+        state, hidden = run_kernel(
+            forward_kernel,
+            (narrow, wide),
+            conv_flops + cell_flops,
+            rims(state, radius),
+            tap_tiles(conv_kernel[layer]),
+            mask_wide,
+            gains[layer],
             expand_weight[layer],
             project_weight[layer],
-        )
-        state = (state.astype(jnp.float32) + mask_value[:, :, None] * update).astype(jnp.bfloat16)
-    cotangent = ocean_cotangent.astype(jnp.float32)
-    for layer in range(layer_count - 1, -1, -1):
-        hidden = depthwise(windows[layer], conv_kernel[layer])
-        hidden_adjoint = cell_backward(
-            hidden,
-            norm_gain[layer],
+            scratch=window_scratch,
+        )
+        hiddens.append(hidden)
+
+    def cell_operands(layer):
+        return (
+            mask_wide,
+            gains[layer],
             expand_weight[layer],
-            project_weight[layer],
-            mask_value,
+            expand_weight[layer].T,
+            project_weight[layer].T,
+        )
+
+    def conv_operands(layer, adjoint):
+        return (
+            rims(adjoint, radius),
+            tap_tiles(conv_kernel[layer, ::-1, ::-1]),
+        )
+
+    last = layer_count - 1
+    cotangent = ocean_cotangent
+    hidden_adjoint = run_kernel(
+        backward_kernel,
+        narrow,
+        2 * cell_flops,
+        hiddens[last],
+        cotangent,
+        *cell_operands(last),
+    )
+    for layer in range(last, 0, -1):
+        cotangent, hidden_adjoint = run_kernel(
+            adjoint_backward_kernel,
+            (wide, narrow),
+            conv_flops + 2 * cell_flops,
+            *conv_operands(layer, hidden_adjoint),
             cotangent,
-        )
-        cotangent = cotangent + depthwise(
-            rims(hidden_adjoint, radius), conv_kernel[layer, ::-1, ::-1]
-        )
+            hiddens[layer - 1],
+            *cell_operands(layer - 1),
+            scratch=window_scratch,
+        )
+    cotangent = run_kernel(
+        adjoint_kernel,
+        wide,
+        conv_flops,
+        *conv_operands(0, hidden_adjoint),
+        cotangent,
+        scratch=window_scratch,
+    )
     forcing_adjoint = (
         (mask_value[:, :, None] * cotangent)
         .reshape(ocean_rows, half, ratio, ocean_channels)
@@ -283,9 +432,12 @@
     flux_ocean_adjoint = jnp.einsum(
         "ogc,fc->ogf", forcing_adjoint, flux_embed.astype(jnp.float32), precision=highest
     )
-    full_adjoint = place_half(flux_ocean_adjoint, lon_count, offset)
-    flux_adjoint = spread_rows(to_ocean.T, full_adjoint.reshape(ocean_rows, lon_count * flux_count))
-    flux_adjoint = flux_adjoint.reshape(lat_rows, lon_count, flux_count)
+    flux_parts = jnp.dot(
+        to_ocean.T, flux_ocean_adjoint.reshape(ocean_rows, flux_width), precision=highest
+    )
+    flux_adjoint = sum_halves(
+        swap(flux_parts.reshape(band_total, lat_rows, flux_width)), sections
+    ).reshape(lat_rows, lon_count, flux_count)
     from_flux = jnp.einsum(
         "agf,cf->agc", flux_adjoint, flux_read.astype(jnp.float32), precision=highest
     )
@@ -305,7 +457,11 @@
     )
     atmosphere_grad = input_adjoint + from_flux
     surface_adjoint = jnp.einsum("agc,c->ag", input_adjoint, surface_embed, precision=highest)
-    coarse_adjoint = collect_rows(to_atmosphere.T, surface_adjoint, lon_count, 1, offset, half)
+    coarse_adjoint = jnp.dot(
+        to_atmosphere.T,
+        swap(for_halves(surface_adjoint, sections)).reshape(lat_count, half),
+        precision=highest,
+    )
     widened_adjoint = jnp.broadcast_to(
         coarse_adjoint[:, :, None], (ocean_rows, half, ratio)
     ).reshape(ocean_rows, ocean_lon)

time: 683 us -> 316 us (0.46)
  other arithmetic: 217 us -> 31.4 us
  blocking collectives: 130 us -> 10.7 us
  Pallas kernels: 0 us -> 116 us
  waiting for transfers between devices: 121 us -> 12.4 us
  matrix products: 75.4 us -> 19.9 us
  between operations: 17.5 us -> 1.54 us
  starting transfers between devices: 53.5 us -> 67.7 us
    unnamed x2 -> x0, waiting for transfers between devices: 118 us -> none
    pallas_call x0 -> x5, Pallas kernels: none -> 116 us  [run_kernel(): pl.pallas_call(kernel, out_shape=outs, in_specs=[pl.BlockSpec(memory_spac...]
    unnamed x2 -> x0, blocking collectives: 85.8 us -> none
    add x1 -> x0, other arithmetic: 62.1 us -> none  [per_device(): cotangent + depthwise(rims(hidden_adjoint, radius), conv_kernel[layer, ::...]
    add x1, other arithmetic: 61.6 us -> 4.94 us  [per_device(): cotangent + surface_grad[:, :, None] * surface_read.astype(jnp.float32)[N...]
    dot_general x10 -> x4, matrix products: 53.5 us -> 2.28 us  [the longest x1 1.27 us: per_device(): jnp.dot(to_ocean, arrived[:, :, :flux_width].reshape(lat_count, flux_widt...]
    reduce_sum x4 -> x2, other arithmetic: 45.6 us -> 0.07 us  [sum_halves(): received.reshape(sections, count // sections, lat_rows, width).sum(axis=1)]
    all_gather x1 -> x0, blocking collectives: 44.3 us -> none  [collect_rows(): piece = lax.all_gather(values, ('sec', 'tile'), axis=0, tiled=True)]
  transfers between devices with their start and end apart: 21 -> 22, of which waited for: 4 -> 5; matrix products, arithmetic and copies ran while one was open for 37% -> 25% of each run, Pallas kernels for 0% -> 31%
where the time goes in v1:
time: 316 us; the launch traced here: 314 us
  Pallas kernels  116 us (37%)
  starting transfers between devices  67.7 us (21%)
  local copies, waits for them, and re-layouts  55.2 us (17%)
  other arithmetic  31.4 us (10%)
  matrix products  19.9 us (6%)
  waiting for transfers between devices  12.4 us (4%)
  blocking collectives  10.7 us (3%)
    pallas_call x5, Pallas kernels, run_kernel(): pl.pallas_call(kernel, out_shape=outs, in_specs=[pl.BlockSpec(memory_spac...  116 us
    unnamed x88, local copies, waits for them, and re-layouts  18.7 us
    all_to_all x2, starting transfers between devices, to_bands(): lax.all_to_all(values, ('sec', 'tile'), split_axis=0, concat_axis=1, tile...  18.4 us
    ppermute x8, starting transfers between devices, with_halo(): before = lax.ppermute(last, axis, up)  15.4 us
    all_to_all x2, starting transfers between devices, swap(): lax.all_to_all(values, ('sec', 'tile'), split_axis=0, concat_axis=0, tile...  14.7 us
    concatenate x4, other arithmetic, with_halo(): x = jnp.concatenate([before, x, after], axis=dim)  11.4 us
    all_to_all x1, blocking collectives, swap(): lax.all_to_all(values, ('sec', 'tile'), split_axis=0, concat_axis=0, tile...  10.7 us
    all_to_all x2, starting transfers between devices, to_modes(): lax.all_to_all(values, ('sec', 'tile'), split_axis=1, concat_axis=0, tile...  10.6 us
  transfers between devices with their start and end apart: 22, of which 5 were waited for; matrix products, arithmetic and copies ran while one was open for 25% of the time, Pallas kernels for 31%

profile of v1, /device:TPU:0, one launch (start us, length us, event | category | flops | bytes accessed | tf_op | source)
XLA Modules:
  0.0 314.4 jit_solution(5274347039851274455)
XLA Ops:
  6.8 7.3 %all-to-all-start = ((f32[32,1,1620]{2,1,0:T(1,128)}), f32[32,1,1620]{2,1,0:T(1,128)S(1)}, u32[]{:S(2)}, u32[]{:S(2)}) async-start(f32[32,1,1620]{2,1,0:T(1,128)} %copy.133), calls=%async_computation | async-start | bytes 425984 | tf_op jit(solution)/shard_map/all_to_all | solution.py:256
  19.8 3.5 %all-to-all-done = f32[32,1,1620]{2,1,0:T(1,128)S(1)} async-done(((f32[32,1,1620]{2,1,0:T(1,128)}), f32[32,1,1620]{2,1,0:T(1,128)S(1)}, u32[]{:S(2)}, u32[]{:S(2)}) %all-to-all-start) | async-done | bytes 207392 | tf_op jit(solution)/shard_map/all_to_all | solution.py:256
  27.9 3.3 %all-to-all-start.1 = ((bf16[32,2,1536]{2,1,0:T(2,128)(2,1)}), bf16[32,2,1536]{2,1,0:T(2,128)(2,1)}, u32[]{:S(2)}, u32[]{:S(2)}) async-start(bf16[32,2,1536]{2,1,0:T(2,128)(2,1)} %reshape.424), calls=%async_computation.1 | async-start | bytes 393216 | tf_op jit(solution)/shard_map/all_to_all | solution.py:243
  35.9 2.3 collective-permute-start
  40.1 2.2 reshape.425
  42.4 2.8 bitcast_reduce_fusion.1
  52.5 9.1 %all-to-all-start.2 = ((bf16[32,8,384]{2,1,0:T(8,128)(2,1)}), bf16[32,8,384]{2,1,0:T(8,128)(2,1)}, u32[]{:S(2)}, u32[]{:S(2)}) async-start(bf16[32,8,384]{2,1,0:T(8,128)(2,1)} %copy.139), calls=%async_computation.2 | async-start | bytes 393216 | tf_op jit(solution)/shard_map/all_to_all | solution.py:247
  61.6 3.9 %pad_maximum_fusion.narrow = bf16[14,726,128]{2,1,0:T(8,128)(2,1)} fusion(bf16[14,3,128]{2,1,0:T(4,128)(2,1)} %collective-permute-done.3, bf16[3,720,128]{2,1,0:T(8,128)(2,1)S(1)} %collective-permute-done.1, bf16[8,720,128]{2,1,0:T(8,128)(2,1)S(1)} %add_convert_fusion, bf16[3,720,128]{2,1,0:T(8,128)(2,1)S(1)} %collective-permute-done, ...), kind=kLoop, calls=%fused_computation.2 | loop fusion | flops 13009920 | bytes 5203968 | tf_op jit(solution)/shard_map/concatenate | solution.py:18
  68.0 26.0 %shard_map.210 = (bf16[8,720,128]{2,1,0:T(8,128)(2,1)}, f32[8,720,128]{2,1,0:T(8,128)}) custom-call(bf16[14,726,128]{2,1,0:T(8,128)(2,1)} %pad_maximum_fusion.narrow, f32[49,8,128]{2,1,0:T(8,128)} %broadcast_in_dim.26.taps, bf16[8,720,128]{2,1,0:T(8,128)(2,1)} %mul.198.mask, f32[1,128]{1,0:T(1,128)} %get-tuple-element.49.gain, ...), custom_call_target="tpu_custom_call" | custom-call | flops 4494458880 | bytes 4539904 | tf_op jit(solution)/shard_map/pallas_call | solution.py:162
  96.1 2.9 collective-permute-start.4
  110.9 2.2 add_convert_fusion.1
  121.9 3.4 %reduce.15 = bf16[256,384]{1,0:T(8,128)(2,1)} reduce(bf16[256,1,384]{2,1,0:T(2,128)(2,1)} %bitcast.205, bf16[]{:T(256)} %broadcast.210), dimensions={1}, to_apply=%bitcast.177.reduce_sub_computation | reduce | bytes 393218
  127.0 7.3 %all-to-all-start.3 = ((bf16[32,2,1536]{2,1,0:T(2,128)(2,1)}), bf16[32,2,1536]{2,1,0:T(2,128)(2,1)}, u32[]{:S(2)}, u32[]{:S(2)}) async-start(bf16[32,2,1536]{2,1,0:T(2,128)(2,1)} %reshape.426), calls=%async_computation.3 | async-start | bytes 393216 | tf_op jit(solution)/shard_map/all_to_all | solution.py:243
  134.3 2.2 pad_maximum_fusion.1.narrow
  137.2 26.0 %shard_map.211 = (bf16[8,720,128]{2,1,0:T(8,128)(2,1)}, f32[8,720,128]{2,1,0:T(8,128)}) custom-call(bf16[14,726,128]{2,1,0:T(8,128)(2,1)} %pad_maximum_fusion.1.narrow, f32[49,8,128]{2,1,0:T(8,128)} %broadcast_in_dim.27.taps, bf16[8,720,128]{2,1,0:T(8,128)(2,1)} %mul.198.mask, f32[1,128]{1,0:T(1,128)} %get-tuple-element.48.gain, ...), custom_call_target="tpu_custom_call" | custom-call | flops 4494458880 | bytes 4539904 | tf_op jit(solution)/shard_map/pallas_call | solution.py:162
  163.1 14.6 %shard_map.212 = bf16[8,720,128]{2,1,0:T(8,128)(2,1)} custom-call(f32[8,720,128]{2,1,0:T(8,128)} %get-tuple-element.12.hidden, bf16[8,720,128]{2,1,0:T(8,128)(2,1)} %cotangent.3, bf16[8,720,128]{2,1,0:T(8,128)(2,1)} %mul.198.mask, f32[1,128]{1,0:T(1,128)} %get-tuple-element.48.gain, bf16[128,512]{1,0:T(8,128)(2,1)} %get-tuple-element.42.expand, ...), custom_call_target="tpu_custom_call" | custom-call | flops 6039797760 | bytes 6291968 | tf_op jit(solution)/shard_map/pallas_call | solution.py:162
  177.7 2.3 fusion.98
  180.0 2.2 collective-permute-start.8
  183.8 2.2 reshape.427
  186.0 2.8 bitcast_reduce_fusion
  195.8 9.3 %all-to-all-start.4 = ((bf16[32,8,384]{2,1,0:T(8,128)(2,1)}), bf16[32,8,384]{2,1,0:T(8,128)(2,1)}, u32[]{:S(2)}, u32[]{:S(2)}) async-start(bf16[32,8,384]{2,1,0:T(8,128)(2,1)} %copy.156), calls=%async_computation.4 | async-start | bytes 393216 | tf_op jit(solution)/shard_map/all_to_all | solution.py:247
  205.1 3.2 %pad_maximum_fusion.2.narrow = bf16[14,726,128]{2,1,0:T(8,128)(2,1)} fusion(bf16[14,3,128]{2,1,0:T(4,128)(2,1)S(1)} %collective-permute-done.11, bf16[3,720,128]{2,1,0:T(8,128)(2,1)S(1)} %collective-permute-done.9, bf16[8,720,128]{2,1,0:T(8,128)(2,1)S(1)} %copy-done.1, bf16[3,720,128]{2,1,0:T(8,128)(2,1)S(1)} %collective-permute-done.8, ...), kind=kLoop, calls=%fused_computation.4 | loop fusion | flops 13009920 | bytes 5203968 | tf_op jit(solution)/shard_map/concatenate | solution.py:18
  209.0 30.4 %shard_map.213 = (f32[8,720,128]{2,1,0:T(8,128)}, bf16[8,720,128]{2,1,0:T(8,128)(2,1)}) custom-call(bf16[14,726,128]{2,1,0:T(8,128)(2,1)} %pad_maximum_fusion.2.narrow, f32[49,8,128]{2,1,0:T(8,128)} %broadcast_in_dim.28.taps, bf16[8,720,128]{2,1,0:T(8,128)(2,1)} %cotangent.3, f32[8,720,128]{2,1,0:T(8,128)} %get-tuple-element.13.hidden, ...), custom_call_target="tpu_custom_call" | custom-call | flops 7514357760 | bytes 9094656 | tf_op jit(solution)/shard_map/pallas_call | solution.py:162
  239.5 2.1 fusion.97
  241.6 3.0 collective-permute-start.12
  248.6 7.4 %all-to-all-start.6 = ((f32[32,1,180]{2,1,0:T(1,128)}), f32[32,1,180]{2,1,0:T(1,128)S(1)}, u32[]{:S(2)}, u32[]{:S(2)}) async-start(f32[32,1,180]{2,1,0:T(1,128)} %broadcast_in_dim.31), calls=%async_computation.6 | async-start | bytes 65536 | tf_op jit(solution)/shard_map/all_to_all | solution.py:256
  256.6 6.5 %all-to-all-done.6 = f32[32,1,180]{2,1,0:T(1,128)S(1)} async-done(((f32[32,1,180]{2,1,0:T(1,128)}), f32[32,1,180]{2,1,0:T(1,128)S(1)}, u32[]{:S(2)}, u32[]{:S(2)}) %all-to-all-start.6) | async-done | bytes 23072 | tf_op jit(solution)/shard_map/all_to_all | solution.py:256
  270.5 2.2 pad_maximum_fusion.3.narrow
  273.3 18.7 %shard_map.214 = f32[8,720,128]{2,1,0:T(8,128)} custom-call(bf16[14,726,128]{2,1,0:T(8,128)(2,1)} %pad_maximum_fusion.3.narrow, f32[49,8,128]{2,1,0:T(8,128)} %broadcast_in_dim.29.taps, f32[8,720,128]{2,1,0:T(8,128)} %get-tuple-element.15.cotangent), custom_call_target="tpu_custom_call" | custom-call | flops 1474560000 | bytes 5751808 | tf_op jit(solution)/shard_map/pallas_call | solution.py:162
  292.0 4.9 %multiply_add_fusion = (f32[8,720,128]{2,1,0:T(8,128)}, f32[8,720,128]{2,1,0:T(8,128)S(1)}) fusion(f32[8,720,128]{2,1,0:T(8,128)} %shard_map.214, f32[128]{0:T(128)S(1)} %copy-done.32, f32[8,720]{1,0:T(8,128)} %multiply_multiply_fusion.2, f32[8,720]{1,0:T(8,128)} %copy-done.14), kind=kLoop, calls=%fused_computation | loop fusion | flops 2211840 | bytes 8893952 | tf_op jit(solution)/shard_map/add | solution.py:470
  297.0 2.9 reduce_sum.38
  302.3 10.7 %all_to_all.51 = f32[32,1,1440]{2,1,0:T(1,128)S(1)} all-to-all(f32[32,1,1440]{2,1,0:T(1,128)S(1)} %copy.160), channel_id=1, replica_groups=mesh['sec'=2,'tile'=16] {'sec','tile'}, dimensions={0} | all-to-all | bytes 368640 | tf_op jit(solution)/shard_map/all_to_all | solution.py:256
  (206 shorter events, 83.1 us)
Async XLA Ops:
  0.6 50.9 %copy-start = (bf16[4,32,32]{2,1,0:T(8,128)(2,1)S(1)}, bf16[4,32,32]{2,1,0:T(8,128)(2,1)}, u32[]{:S(2)}) copy-start(bf16[4,32,32]{2,1,0:T(8,128)(2,1)} %param.30) | copy-start | bytes 24580
  6.8 16.5 %all-to-all-start = ((f32[32,1,1620]{2,1,0:T(1,128)}), f32[32,1,1620]{2,1,0:T(1,128)S(1)}, u32[]{:S(2)}, u32[]{:S(2)}) async-start(f32[32,1,1620]{2,1,0:T(1,128)} %copy.133), calls=%async_computation | async-start | bytes 425984 | tf_op jit(solution)/shard_map/all_to_all | solution.py:256
  14.8 19.1 %copy-start.14 = (f32[8,720]{1,0:T(8,128)}, f32[8,720]{1,0:T(8,128)S(1)}, u32[]{:S(2)}) copy-start(f32[8,720]{1,0:T(8,128)S(1)} %get-tuple-element.47) | copy-start | bytes 69124
  15.8 15.5 %copy-start.21 = (f32[32,8]{0,1:T(8,128)}, f32[32,8]{0,1:T(8,128)S(1)}, u32[]{:S(2)}) copy-start(f32[32,8]{0,1:T(8,128)S(1)} %fusion.80) | copy-start | bytes 3076
  27.9 12.2 %all-to-all-start.1 = ((bf16[32,2,1536]{2,1,0:T(2,128)(2,1)}), bf16[32,2,1536]{2,1,0:T(2,128)(2,1)}, u32[]{:S(2)}, u32[]{:S(2)}) async-start(bf16[32,2,1536]{2,1,0:T(2,128)(2,1)} %reshape.424), calls=%async_computation.1 | async-start | bytes 393216 | tf_op jit(solution)/shard_map/all_to_all | solution.py:243
  35.9 12.9 %collective-permute-start = (bf16[3,720,128]{2,1,0:T(8,128)(2,1)}, bf16[3,720,128]{2,1,0:T(8,128)(2,1)S(1)}, u32[]{:S(2)}, u32[]{:S(2)}) collective-permute-start(bf16[3,720,128]{2,1,0:T(8,128)(2,1)} %get-tuple-element.34), channel_id=1, source_target_pairs={{0,1},{1,2},{2,3},{3,4},{4,5},{5,6},{6,7},{7,8},{8,9},{9,10},{10,1... | collective-permute-start | bytes 1658888 | tf_op jit(solution)/shard_map/ppermute | solution.py:16
  38.2 10.7 %collective-permute-start.1 = (bf16[3,720,128]{2,1,0:T(8,128)(2,1)}, bf16[3,720,128]{2,1,0:T(8,128)(2,1)S(1)}, u32[]{:S(2)}, u32[]{:S(2)}) collective-permute-start(bf16[3,720,128]{2,1,0:T(8,128)(2,1)} %get-tuple-element.35), channel_id=1, source_target_pairs={{1,0},{2,1},{3,2},{4,3},{5,4},{6,5},{7,6},{8,7},{9,8},{10,9},{11,1... | collective-permute-start | bytes 1658888 | tf_op jit(solution)/shard_map/ppermute | solution.py:17
  49.5 12.1 %collective-permute-start.2 = (bf16[14,3,128]{2,1,0:T(4,128)(2,1)}, bf16[14,3,128]{2,1,0:T(4,128)(2,1)}, u32[]{:S(2)}, u32[]{:S(2)}) collective-permute-start(bf16[14,3,128]{2,1,0:T(4,128)(2,1)} %get-tuple-element.26), channel_id=1, source_target_pairs={{0,16},{16,0},{1,17},{17,1},{2,18},{18,2},{3,19},{19,3},{4,20},{20... | collective-permute-start | bytes 32264 | tf_op jit(solution)/shard_map/ppermute | solution.py:16
  50.5 11.1 %collective-permute-start.3 = (bf16[14,3,128]{2,1,0:T(4,128)(2,1)}, bf16[14,3,128]{2,1,0:T(4,128)(2,1)}, u32[]{:S(2)}, u32[]{:S(2)}) collective-permute-start(bf16[14,3,128]{2,1,0:T(4,128)(2,1)} %get-tuple-element.27), channel_id=1, source_target_pairs={{16,0},{0,16},{17,1},{1,17},{18,2},{2,18},{19,3},{3,19},{20,4},{4,... | collective-permute-start | bytes 32264 | tf_op jit(solution)/shard_map/ppermute | solution.py:17
  52.5 58.4 %all-to-all-start.2 = ((bf16[32,8,384]{2,1,0:T(8,128)(2,1)}), bf16[32,8,384]{2,1,0:T(8,128)(2,1)}, u32[]{:S(2)}, u32[]{:S(2)}) async-start(bf16[32,8,384]{2,1,0:T(8,128)(2,1)} %copy.139), calls=%async_computation.2 | async-start | bytes 393216 | tf_op jit(solution)/shard_map/all_to_all | solution.py:247
  96.1 18.2 %copy-start.5 = (bf16[8,720,128]{2,1,0:T(8,128)(2,1)S(1)}, bf16[8,720,128]{2,1,0:T(8,128)(2,1)}, u32[]{:S(2)}) copy-start(bf16[8,720,128]{2,1,0:T(8,128)(2,1)} %get-tuple-element.10) | copy-start | bytes 4423684
  96.1 17.1 %collective-permute-start.4 = (bf16[3,720,128]{2,1,0:T(8,128)(2,1)}, bf16[3,720,128]{2,1,0:T(8,128)(2,1)}, u32[]{:S(2)}, u32[]{:S(2)}) collective-permute-start(bf16[3,720,128]{2,1,0:T(8,128)(2,1)} %get-tuple-element.33), channel_id=1, source_target_pairs={{0,1},{1,2},{2,3},{3,4},{4,5},{5,6},{6,7},{7,8},{8,9},{9,10},{10,1... | collective-permute-start | bytes 1658888 | tf_op jit(solution)/shard_map/ppermute | solution.py:16
  98.9 15.6 %collective-permute-start.5 = (bf16[3,720,128]{2,1,0:T(8,128)(2,1)S(1)}, bf16[3,720,128]{2,1,0:T(8,128)(2,1)S(1)}, u32[]{:S(2)}, u32[]{:S(2)}) collective-permute-start(bf16[3,720,128]{2,1,0:T(8,128)(2,1)S(1)} %get-tuple-element.32), channel_id=1, source_target_pairs={{1,0},{2,1},{3,2},{4,3},{5,4},{6,5},{7,6},{8,7},{9,8},{10,9},{11,1... | collective-permute-start | bytes 1658888 | tf_op jit(solution)/shard_map/ppermute | solution.py:17
  116.7 17.6 %collective-permute-start.6 = (bf16[14,3,128]{2,1,0:T(4,128)(2,1)}, bf16[14,3,128]{2,1,0:T(4,128)(2,1)S(1)}, u32[]{:S(2)}, u32[]{:S(2)}) collective-permute-start(bf16[14,3,128]{2,1,0:T(4,128)(2,1)} %get-tuple-element.24), channel_id=1, source_target_pairs={{0,16},{16,0},{1,17},{17,1},{2,18},{18,2},{3,19},{19,3},{4,20},{20... | collective-permute-start | bytes 32264 | tf_op jit(solution)/shard_map/ppermute | solution.py:16
  118.3 15.9 %collective-permute-start.7 = (bf16[14,3,128]{2,1,0:T(4,128)(2,1)}, bf16[14,3,128]{2,1,0:T(4,128)(2,1)S(1)}, u32[]{:S(2)}, u32[]{:S(2)}) collective-permute-start(bf16[14,3,128]{2,1,0:T(4,128)(2,1)} %get-tuple-element.25), channel_id=1, source_target_pairs={{16,0},{0,16},{17,1},{1,17},{18,2},{2,18},{19,3},{3,19},{20,4},{4,... | collective-permute-start | bytes 32264 | tf_op jit(solution)/shard_map/ppermute | solution.py:17
  118.7 15.6 %copy-start.7 = (bf16[14,720,128]{2,1,0:T(8,128)(2,1)S(1)}, bf16[14,720,128]{2,1,0:T(8,128)(2,1)}, u32[]{:S(2)}) copy-start(bf16[14,720,128]{2,1,0:T(8,128)(2,1)} %copy-done.6) | copy-start | bytes 7741444
  127.0 56.8 %all-to-all-start.3 = ((bf16[32,2,1536]{2,1,0:T(2,128)(2,1)}), bf16[32,2,1536]{2,1,0:T(2,128)(2,1)}, u32[]{:S(2)}, u32[]{:S(2)}) async-start(bf16[32,2,1536]{2,1,0:T(2,128)(2,1)} %reshape.426), calls=%async_computation.3 | async-start | bytes 393216 | tf_op jit(solution)/shard_map/all_to_all | solution.py:243
  180.0 12.7 %collective-permute-start.8 = (bf16[3,720,128]{2,1,0:T(8,128)(2,1)}, bf16[3,720,128]{2,1,0:T(8,128)(2,1)S(1)}, u32[]{:S(2)}, u32[]{:S(2)}) collective-permute-start(bf16[3,720,128]{2,1,0:T(8,128)(2,1)} %get-tuple-element.30), channel_id=1, source_target_pairs={{0,1},{1,2},{2,3},{3,4},{4,5},{5,6},{6,7},{7,8},{8,9},{9,10},{10,1... | collective-permute-start | bytes 1658888 | tf_op jit(solution)/shard_map/ppermute | solution.py:16
  182.3 10.4 %collective-permute-start.9 = (bf16[3,720,128]{2,1,0:T(8,128)(2,1)}, bf16[3,720,128]{2,1,0:T(8,128)(2,1)S(1)}, u32[]{:S(2)}, u32[]{:S(2)}) collective-permute-start(bf16[3,720,128]{2,1,0:T(8,128)(2,1)} %get-tuple-element.31), channel_id=1, source_target_pairs={{1,0},{2,1},{3,2},{4,3},{5,4},{6,5},{7,6},{8,7},{9,8},{10,9},{11,1... | collective-permute-start | bytes 1658888 | tf_op jit(solution)/shard_map/ppermute | solution.py:17
  192.7 12.4 %collective-permute-start.10 = (bf16[14,3,128]{2,1,0:T(4,128)(2,1)S(1)}, bf16[14,3,128]{2,1,0:T(4,128)(2,1)S(1)}, u32[]{:S(2)}, u32[]{:S(2)}) collective-permute-start(bf16[14,3,128]{2,1,0:T(4,128)(2,1)S(1)} %get-tuple-element.22), channel_id=1, source_target_pairs={{0,16},{16,0},{1,17},{17,1},{2,18},{18,2},{3,19},{19,3},{4,20},{20... | collective-permute-start | bytes 32264 | tf_op jit(solution)/shard_map/ppermute | solution.py:16
  194.4 10.7 %collective-permute-start.11 = (bf16[14,3,128]{2,1,0:T(4,128)(2,1)S(1)}, bf16[14,3,128]{2,1,0:T(4,128)(2,1)S(1)}, u32[]{:S(2)}, u32[]{:S(2)}) collective-permute-start(bf16[14,3,128]{2,1,0:T(4,128)(2,1)S(1)} %get-tuple-element.23), channel_id=1, source_target_pairs={{16,0},{0,16},{17,1},{1,17},{18,2},{2,18},{19,3},{3,19},{20,4},{4,... | collective-permute-start | bytes 32264 | tf_op jit(solution)/shard_map/ppermute | solution.py:17
  195.8 48.8 %all-to-all-start.4 = ((bf16[32,8,384]{2,1,0:T(8,128)(2,1)}), bf16[32,8,384]{2,1,0:T(8,128)(2,1)}, u32[]{:S(2)}, u32[]{:S(2)}) async-start(bf16[32,8,384]{2,1,0:T(8,128)(2,1)} %copy.156), calls=%async_computation.4 | async-start | bytes 393216 | tf_op jit(solution)/shard_map/all_to_all | solution.py:247
  209.0 35.6 %copy-start.10 = (bf16[1,360,384]{2,1,0:T(8,128)(2,1)S(1)}, bf16[1,360,384]{2,1,0:T(8,128)(2,1)}, u32[]{:S(2)}) copy-start(bf16[1,360,384]{2,1,0:T(8,128)(2,1)} %param.36) | copy-start | bytes 829444
  239.5 16.6 %copy-start.31 = (bf16[128]{0:T(256)(128)(2,1)S(1)}, bf16[128]{0:T(256)(128)(2,1)}, u32[]{:S(2)}) copy-start(bf16[128]{0:T(256)(128)(2,1)} %param.25) | copy-start | bytes 772
  239.5 23.6 %copy-start.24 = (f32[32,8]{0,1:T(8,128)S(1)}, f32[32,8]{0,1:T(8,128)}, u32[]{:S(2)}) copy-start(f32[32,8]{0,1:T(8,128)} %copy-done.23) | copy-start | bytes 3076
  241.6 23.1 %copy-start.4 = (bf16[8,720,128]{2,1,0:T(8,128)(2,1)S(1)}, bf16[8,720,128]{2,1,0:T(8,128)(2,1)}, u32[]{:S(2)}) copy-start(bf16[8,720,128]{2,1,0:T(8,128)(2,1)} %get-tuple-element.14) | copy-start | bytes 4423684
  241.6 22.0 %collective-permute-start.12 = (bf16[3,720,128]{2,1,0:T(8,128)(2,1)}, bf16[3,720,128]{2,1,0:T(8,128)(2,1)}, u32[]{:S(2)}, u32[]{:S(2)}) collective-permute-start(bf16[3,720,128]{2,1,0:T(8,128)(2,1)} %get-tuple-element.29), channel_id=1, source_target_pairs={{0,1},{1,2},{2,3},{3,4},{4,5},{5,6},{6,7},{7,8},{8,9},{9,10},{10,1... | collective-permute-start | bytes 1658888 | tf_op jit(solution)/shard_map/ppermute | solution.py:16
  245.9 19.0 %collective-permute-start.13 = (bf16[3,720,128]{2,1,0:T(8,128)(2,1)S(1)}, bf16[3,720,128]{2,1,0:T(8,128)(2,1)}, u32[]{:S(2)}, u32[]{:S(2)}) collective-permute-start(bf16[3,720,128]{2,1,0:T(8,128)(2,1)S(1)} %get-tuple-element.28), channel_id=1, source_target_pairs={{1,0},{2,1},{3,2},{4,3},{5,4},{6,5},{7,6},{8,7},{9,8},{10,9},{11,1... | collective-permute-start | bytes 1658888 | tf_op jit(solution)/shard_map/ppermute | solution.py:17
  248.6 14.4 %all-to-all-start.6 = ((f32[32,1,180]{2,1,0:T(1,128)}), f32[32,1,180]{2,1,0:T(1,128)S(1)}, u32[]{:S(2)}, u32[]{:S(2)}) async-start(f32[32,1,180]{2,1,0:T(1,128)} %broadcast_in_dim.31), calls=%async_computation.6 | async-start | bytes 65536 | tf_op jit(solution)/shard_map/all_to_all | solution.py:256
  266.1 3.8 %collective-permute-start.14 = (bf16[14,3,128]{2,1,0:T(4,128)(2,1)S(1)}, bf16[14,3,128]{2,1,0:T(4,128)(2,1)S(1)}, u32[]{:S(2)}, u32[]{:S(2)}) collective-permute-start(bf16[14,3,128]{2,1,0:T(4,128)(2,1)S(1)} %get-tuple-element.20), channel_id=1, source_target_pairs={{0,16},{16,0},{1,17},{17,1},{2,18},{18,2},{3,19},{19,3},{4,20},{20... | collective-permute-start | bytes 32264 | tf_op jit(solution)/shard_map/ppermute | solution.py:16
  266.8 3.7 %collective-permute-start.15 = (bf16[14,3,128]{2,1,0:T(4,128)(2,1)S(1)}, bf16[14,3,128]{2,1,0:T(4,128)(2,1)S(1)}, u32[]{:S(2)}, u32[]{:S(2)}) collective-permute-start(bf16[14,3,128]{2,1,0:T(4,128)(2,1)S(1)} %get-tuple-element.21), channel_id=1, source_target_pairs={{16,0},{0,16},{17,1},{1,17},{18,2},{2,18},{19,3},{3,19},{20,4},{4,... | collective-permute-start | bytes 32264 | tf_op jit(solution)/shard_map/ppermute | solution.py:17
  273.3 18.7 %copy-start.32 = (f32[128]{0:T(128)S(1)}, f32[128]{0:T(128)}, u32[]{:S(2)}) copy-start(f32[128]{0:T(128)} %convert_element_type.197) | copy-start | bytes 1540
  (26 other events, 227.5 us)
